TPU v7x, 32 devices: a whole 2x2x4 slice. The times are simulated.
32 devices in a mesh: row: 8 (over z, y), col: 4 (over x, core).
Axes of the slice: x: 2, y: 2, z: 4, core: 2. Of those that a mesh axis runs over, the one named last changes fastest.
Arguments:
- matrix: float32 [4, 8, 512, 8, 4, 512], P(None, 'row', None, None, 'col'), may hold values from -30 to 30, as said below
Outputs:
- factored: float32 [4, 8, 512, 8, 4, 512], P(None, 'row', None, None, 'col')
Inputs may be any that keep to these rules, and one draw needn't show every extreme that they name: matrix is symmetric, positive definite and well conditioned.
All inputs are finite; a program needn't handle non-finite values.
Results may differ from a plain program's by a relative error of at most 0.00013.
Values sent between devices are 32-bit elements; how exact they have to be, the bound alone decides.
A program may use at most 192 MiB of HBM per device.

v0:
```python
import jax
import jax.numpy as jnp
from jax import lax
from jax.sharding import PartitionSpec as P

NB = 512
STEPS = 2


def spread(value, axis, source):
    kept = jnp.where(lax.axis_index(axis) == source, value, 0).astype(value.dtype)
    return lax.psum(kept, axis)


def trailing_product(column_panel, transposed):
    return jnp.einsum(
        "tan,sbn->tasb",
        column_panel,
        transposed,
        precision=lax.Precision.HIGHEST,
        preferred_element_type=jnp.float32,
    )


def shards(matrix):
    local_rows = matrix.shape[0]
    local_cols = matrix.shape[3]
    blocks = matrix.reshape(local_rows, NB, local_cols, NB)
    row_count = lax.axis_size("row")
    column_count = lax.axis_size("col")
    group_size = row_count // column_count
    row_place = lax.axis_index("row")
    column_place = lax.axis_index("col")
    tile_rows = jnp.arange(local_rows, dtype=jnp.int32) * row_count + row_place
    tile_columns = jnp.arange(local_cols, dtype=jnp.int32) * column_count + column_place
    anchor = jnp.int32(0)
    for step in range(STEPS):
        root_row = step % row_count
        factor_local_row = step // row_count
        root_col = step % column_count
        factor_local_col = step // column_count
        corner = blocks[factor_local_row, :, factor_local_col, :]
        owner = (row_place == root_row) & (column_place == root_col)
        identity = jnp.eye(NB, dtype=jnp.float32)
        chosen = jnp.where(owner, corner, identity)
        factor_local = jnp.linalg.cholesky(chosen)
        factor_diag_block = spread(factor_local, "row", root_row)
        source = blocks[:, :, factor_local_col, :]
        solved = jax.scipy.linalg.solve_triangular(
            factor_diag_block, source.reshape(local_rows * NB, NB).T, lower=True
        ).T
        solved = solved.reshape(local_rows, NB, NB)
        panel_local = jnp.where((tile_rows > step)[:, None, None], solved, 0.0)
        factor_column_panel = spread(panel_local, "col", root_col)
        empty = jnp.zeros((local_rows, group_size, NB, NB), jnp.float32)
        slot_index = row_place // column_count
        holder = row_place % column_count == column_place
        contribution = jnp.where(holder, factor_column_panel, 0.0)
        filled = lax.dynamic_update_slice(
            empty, contribution[:, None], (anchor, slot_index, anchor, anchor)
        )
        gathered = lax.psum(filled, "row")
        transposed = gathered.reshape(local_cols, NB, NB)
        diag_block, column_panel, transposed = (factor_diag_block, factor_column_panel, transposed)
        write_blocks = blocks
        local_row = step // row_count
        local_col = step // column_count
        column_now = write_blocks[:, :, local_col, :]
        owns_col = column_place == step % column_count
        row_after = (tile_rows > step)[:, None, None]
        row_hit = (tile_rows == step)[:, None, None]
        new_column = jnp.where(
            row_after, column_panel, jnp.where(row_hit, diag_block[None], column_now)
        )
        new_column = jnp.where(owns_col, new_column, column_now)
        write_blocks = write_blocks.at[:, :, local_col, :].set(new_column)
        row_now = write_blocks[local_row]
        owns_row = row_place == step % row_count
        zero_cols = (tile_columns > step)[None, :, None]
        new_row = jnp.where(owns_row & zero_cols, 0.0, row_now)
        blocks = write_blocks.at[local_row].set(new_row)
        blocks = blocks - trailing_product(column_panel, transposed)
    return blocks.reshape(matrix.shape)


def solution(mesh):
    in_specs = (P(None, "row", None, None, "col", None),)
    out_specs = P(None, "row", None, None, "col", None)
    return jax.shard_map(shards, mesh=mesh, in_specs=in_specs, out_specs=out_specs, check_vma=False)
```

profile of v0, /device:TPU:0, one launch (start us, length us, event | category | flops | bytes accessed | tf_op | source)
XLA Modules:
  0.0 1563.9 jit_solution(13661579687502120736)
XLA Ops:
  6.5 78.2 %copy.17 = f32[4,1,512,8,1,512]{2,5,3,0,4,1:T(8,128)} copy(f32[4,1,512,8,1,512]{5,4,3,2,1,0:T(1,128)} %param.12) | data formatting | bytes 67108864 | tf_op args[0]
  87.9 11.7 cholesky.286
  99.7 9.8 custom-call.27
  110.3 11.7 cholesky.305
  122.0 10.0 custom-call.28
  132.7 11.7 cholesky.326
  145.2 9.8 custom-call.29
  155.6 11.7 cholesky.343
  182.8 78.7 %copy.42 = f32[4,1,512,8,1,512]{2,5,0,3,1,4:T(8,128)} copy(f32[4,1,512,8,1,512]{5,4,3,2,1,0:T(1,128)} %param.12) | data formatting | bytes 67108864 | tf_op jit(solution)/shard_map/reshape | solution.py:28
  261.6 4.6 slice.220
  266.2 5.3 copy.20
  272.9 7.6 while.8
  280.5 39.3 %custom-call.30 = f32[4,128,128]{1,2,0:T(8,128)S(1)} custom-call(f32[4,128,128]{2,1,0:T(8,128)S(1)} %get-tuple-element.69), custom_call_target="InvertDiagBlocksLowerTriangular" | custom-call | tf_op jit(solution)/shard_map/jit(_solve_triangular)/triangular_solve | solution.py:49
  331.0 5.7 fusion.25
  340.3 5.4 copy.21
  345.7 5.2 copy.22
  350.9 4.9 select_select_fusion.1
  355.9 88.4 %all-reduce.10.cloned.1.call-done = f32[4,512,512]{1,2,0:T(8,128)} async-done(((f32[4,512,512]{1,2,0:T(8,128)}), f32[4,512,512]{1,2,0:T(8,128)}) %all-reduce.10.cloned.1.call-update) | async-done | bytes 4194320 | tf_op jit(solution)/shard_map/psum | solution.py:12
  444.2 4.6 select_bitcast_fusion.1
  448.9 5.3 copy.25
  462.3 6.8 bitcast_dynamic-update-slice_fusion.2
  469.2 8.3 fusion.1
  477.5 253.1 %all-reduce.12.cloned.1.call-done = f32[8,512,512]{2,1,0:T(8,128)} async-done(((f32[8,512,512]{2,1,0:T(8,128)}), f32[8,512,512]{2,1,0:T(8,128)}) %all-reduce.12.cloned.1.call-update) | async-done | bytes 8388624 | tf_op jit(solution)/shard_map/psum | solution.py:62
  730.6 63.0 %convolution_subtract_fusion = f32[4,512,8,512]{1,3,2,0:T(8,128)} fusion(f32[4,512,8,512]{1,3,2,0:T(8,128)} %fusion.1, f32[8,512,512]{2,1,0:T(8,128)} %all-reduce.12.cloned.1.call-done, f32[4,512,512]{1,2,0:T(8,128)} %all-reduce.10.cloned.1.call-done), kind=kOutput, calls=%fused_computation.5 | convolution fusion | flops 51547996160 | bytes 79691776 | tf_op jit(solution)/shard_map/tan,sbn->tasb/dot_general | solution.py:16
  796.7 11.7 cholesky.358
  808.6 9.8 custom-call.31
  819.1 11.7 cholesky.377
  832.2 10.2 custom-call.32
  843.0 11.7 cholesky.398
  855.5 9.8 custom-call.33
  865.9 11.7 cholesky.415
  882.3 6.8 fusion.84
  889.0 5.2 copy.30
  894.3 65.6 %all-reduce.14.cloned.1.call-done = f32[512,512]{1,0:T(8,128)} async-done(((f32[512,512]{1,0:T(8,128)}), f32[512,512]{1,0:T(8,128)}) %all-reduce.14.cloned.1.call-update) | async-done | bytes 1048592 | tf_op jit(solution)/shard_map/psum | solution.py:12
  961.2 7.8 while.9
  969.0 39.3 %custom-call.34 = f32[4,128,128]{1,2,0:T(8,128)S(1)} custom-call(f32[4,128,128]{2,1,0:T(8,128)S(1)} %get-tuple-element.70), custom_call_target="InvertDiagBlocksLowerTriangular" | custom-call | tf_op jit(solution)/shard_map/jit(_solve_triangular)/triangular_solve | solution.py:49
  1019.6 5.6 fusion.22
  1028.7 5.3 copy.31
  1034.0 5.2 copy.32
  1039.3 4.9 select_select_fusion
  1044.2 85.2 %all-reduce.16.cloned.1.call-done = f32[4,512,512]{1,2,0:T(8,128)} async-done(((f32[4,512,512]{1,2,0:T(8,128)}), f32[4,512,512]{1,2,0:T(8,128)}) %all-reduce.16.cloned.1.call-update) | async-done | bytes 4194320 | tf_op jit(solution)/shard_map/psum | solution.py:12
  1129.4 4.6 select_bitcast_fusion
  1134.0 5.3 copy.34
  1147.6 6.8 fusion.6
  1154.4 8.3 fusion
  1162.7 253.0 %all-reduce.18.cloned.1.call-done = f32[8,512,512]{2,1,0:T(8,128)} async-done(((f32[8,512,512]{2,1,0:T(8,128)}), f32[8,512,512]{2,1,0:T(8,128)}) %all-reduce.18.cloned.1.call-update) | async-done | bytes 8388624 | tf_op jit(solution)/shard_map/psum | solution.py:62
  1415.8 62.8 %subtract_bitcast_fusion = f32[4,1,512,8,1,512]{2,5,3,0,4,1:T(8,128)} fusion(f32[4,512,8,512]{1,3,2,0:T(8,128)} %fusion, f32[8,512,512]{2,1,0:T(8,128)} %all-reduce.18.cloned.1.call-done, f32[4,512,512]{1,2,0:T(8,128)} %all-reduce.16.cloned.1.call-done), kind=kOutput, calls=%fused_computation.4 | convolution fusion | flops 51547996160 | bytes 79691776 | tf_op jit(solution)/shard_map/tan,sbn->tasb/dot_general | solution.py:16
  1478.5 78.2 %copy.37 = f32[4,1,512,8,1,512]{5,4,3,2,1,0:T(1,128)} copy(f32[4,1,512,8,1,512]{2,5,3,0,4,1:T(8,128)} %subtract_bitcast_fusion) | data formatting | bytes 67108864 | tf_op jit(solution)/shard_map/reshape | solution.py:83
  (124 shorter events, 81.7 us)
Async XLA Ops:
  6.5 264.9 %all-reduce.8.cloned.1.call-start = ((), (), s32[]{:S(2)}) async-start(), calls=%async_computation | async-start | bytes 2097152 | tf_op jit(solution)/shard_map/psum | solution.py:12
  182.8 261.4 %all-reduce.10.cloned.1.call-start = ((), (), s32[]{:S(2)}) async-start(), calls=%async_computation.1 | async-start | bytes 8388608 | tf_op jit(solution)/shard_map/psum | solution.py:12
  319.8 6.6 copy-start.2
  355.8 374.8 %all-reduce.12.cloned.1.call-start = ((), (), s32[]{:S(2)}) async-start(), calls=%async_computation.2 | async-start | bytes 16777216 | tf_op jit(solution)/shard_map/psum | solution.py:62
  454.1 4.3 copy-start.1
  460.8 1.2 copy-start.4
  460.8 499.0 %all-reduce.14.cloned.1.call-start = ((), (), s32[]{:S(2)}) async-start(), calls=%async_computation.3 | async-start | bytes 2097152 | tf_op jit(solution)/shard_map/psum | solution.py:12
  882.2 247.2 %all-reduce.16.cloned.1.call-start = ((), (), s32[]{:S(2)}) async-start(), calls=%async_computation.4 | async-start | bytes 8388608 | tf_op jit(solution)/shard_map/psum | solution.py:12
  1008.4 6.6 copy-start.3
  1044.2 371.6 %all-reduce.18.cloned.1.call-start = ((), (), s32[]{:S(2)}) async-start(), calls=%async_computation.5 | async-start | bytes 16777216 | tf_op jit(solution)/shard_map/psum | solution.py:62
  1139.3 4.3 copy-start
  1146.0 1.2 copy-start.5
Sparse Core Ops, SparseCore 0:
  182.9 81.0 all-reduce.7
  355.9 88.2 all-reduce.9
  460.9 269.6 all-reduce.11
  882.3 77.4 all-reduce.13
  1044.3 85.0 all-reduce.15
  1146.1 269.5 all-reduce.17
where the time goes:
time: 1580 us; the launch traced here: 1560 us
  waiting for transfers between devices  745 us (47%)
  local copies, waits for them, and re-layouts  321 us (20%)
  other arithmetic  302 us (19%)
  matrix products  165 us (10%)
  between operations  30 us (2%)
    psum x2, waiting for transfers between devices, shards(): gathered = lax.psum(filled, 'row')  506 us
    psum x4, waiting for transfers between devices, spread(): return lax.psum(kept, axis)  239 us
    another operation x29, other arithmetic, shards(): factor_local = jnp.linalg.cholesky(chosen)  158 us
    dot_general x2, matrix products, trailing_product(): jnp.einsum('tan,sbn->tasb', column_panel, transposed, precision=lax.Preci...  126 us
    another operation x5, other arithmetic, shards(): jax.scipy.linalg.solve_triangular(factor_diag_block, source.reshape(local...  81.3 us
    unnamed x13, local copies, waits for them, and re-layouts  80.5 us
    reshape x1, local copies, waits for them, and re-layouts, shards(): blocks = matrix.reshape(local_rows, NB, local_cols, NB)  78.7 us
    reshape x1, local copies, waits for them, and re-layouts, shards(): return blocks.reshape(matrix.shape)  78.2 us
  transfers between devices with their start and end apart: 6, of which 5 were waited for; matrix products, arithmetic and copies ran while one was open for 8% of the time, Pallas kernels for 0%

commit v1 on v0

v1 whole, which is shorter than its diff:
```python
import jax
import jax.numpy as jnp
from jax import lax
from jax.experimental import pallas as pl
from jax.experimental.pallas import tpu as pltpu
from jax.sharding import PartitionSpec as P

NB = 512
STEPS = 2
HIGHEST = lax.Precision.HIGHEST
LANES = 128


def dot_nt(a, b, precision):
    return lax.dot_general(
        a, b, (((1,), (1,)), ((), ())), precision=precision, preferred_element_type=jnp.float32
    )


def factor_tile(work, factor, inverse, pair):
    size = work.shape[0]
    sub = lax.broadcasted_iota(jnp.int32, (LANES, LANES), 0)
    lane = lax.broadcasted_iota(jnp.int32, (LANES, LANES), 1)
    sub_wide = lax.broadcasted_iota(jnp.int32, (LANES, 2 * LANES), 0)
    lane_wide = lax.broadcasted_iota(jnp.int32, (1, 2 * LANES), 1)
    factor[...] = jnp.zeros_like(factor)
    inverse[...] = jnp.zeros_like(inverse)
    for begin in range(0, size, LANES):
        end = begin + LANES
        here = slice(begin, end)
        pair[:, :LANES] = work[here, here]
        pair[:, LANES:] = jnp.where(sub == lane, 1.0, 0.0)

        def eliminate(j, carry):
            row = pair[pl.ds(j, 1), :]
            pivot = jnp.sum(jnp.where(lane_wide == j, row, 0.0), axis=1, keepdims=True)
            scale = 1.0 / jnp.sqrt(pivot)
            row = row * scale
            now = pair[...]
            column = jnp.sum(jnp.where(lane == j, now[:, :LANES], 0.0), axis=1, keepdims=True)
            column = column * scale
            pair[...] = jnp.where(
                sub_wide > j, now - column * row, jnp.where(sub_wide == j, row, now)
            )
            return carry

        lax.fori_loop(0, LANES, eliminate, 0)
        factor[here, here] = jnp.where(sub <= lane, pair[:, :LANES], 0.0).T
        small = jnp.where(sub >= lane, pair[:, LANES:], 0.0)
        if end < size:
            panel = dot_nt(work[end:, here], small, HIGHEST)
            factor[end:, here] = panel
            work[end:, end:] = work[end:, end:] - dot_nt(panel, panel, HIGHEST)
        inverse[here, here] = small
        if begin:
            known = jnp.dot(factor[here, :begin], inverse[:begin, :begin], precision=HIGHEST)
            inverse[here, :begin] = -jnp.dot(small, known, precision=HIGHEST)


def factor_kernel(lead, factor_0, inverse_0, below, factor_1, inverse_1, work, pair):
    work[...] = lead[0]
    factor_tile(work, factor_0, inverse_0, pair)
    solved = dot_nt(lead[1], inverse_0[...], HIGHEST)
    below[...] = solved
    work[...] = lead[2] - dot_nt(solved, solved, HIGHEST)
    factor_tile(work, factor_1, inverse_1, pair)


def factor_lead(lead):
    tile = jax.ShapeDtypeStruct((NB, NB), jnp.float32)
    return pl.pallas_call(
        factor_kernel,
        out_shape=[tile] * 5,
        in_specs=[pl.BlockSpec(memory_space=pltpu.VMEM)],
        out_specs=[pl.BlockSpec(memory_space=pltpu.VMEM)] * 5,
        scratch_shapes=[
            pltpu.VMEM((NB, NB), jnp.float32),
            pltpu.VMEM((LANES, 2 * LANES), jnp.float32),
        ],
        cost_estimate=pl.CostEstimate(flops=10**11, bytes_accessed=10**7, transcendentals=0),
        name="factor_lead",
    )(lead)


def update_kernel(column_count, place, x, row_high, row_low, col_high, col_low, fresh, out):
    rows = row_high.shape[0]
    stride = x.shape[0] // rows
    local_cols = col_high.shape[0] // NB
    p, q = place[0], place[1]
    lead_rows = (pl.program_id(0) * rows < NB) & (p < STEPS)
    high, low = row_high[...], row_low[...]
    for s in range(local_cols):
        tile = slice(s * NB, (s + 1) * NB)
        product = dot_nt(high, col_high[tile, :], None)
        product += dot_nt(high, col_low[tile, :], None)
        product += dot_nt(low, col_high[tile, :], None)
        clear = lead_rows & (s * column_count + q > p)
        for c in range(NB // LANES):
            part = slice(c * LANES, (c + 1) * LANES)
            at = pl.ds(s * (NB // LANES) + c, rows, stride=stride)
            value = x[at, :] - product[:, part]
            if s == 0:
                value = jnp.where(q < STEPS, fresh[:, part], value)
            out[at, :] = jnp.where(clear, 0.0, value)


def split(x):
    high = lax.reduce_precision(x, 8, 7)
    return high.astype(jnp.bfloat16), (x - high).astype(jnp.bfloat16)


def update(place, matrix, row_panel, column_panel, fresh, column_count):
    rows, depth = row_panel.shape
    columns = column_panel.shape[0]
    chunk = 256
    lines = columns // LANES
    flat = matrix.reshape(rows * lines, LANES)
    row_high, row_low = split(row_panel)
    col_high, col_low = split(column_panel)
    whole = pl.BlockSpec((columns, depth), lambda i, _: (0, 0), pipeline_mode=pl.Buffered(1))
    part = pl.BlockSpec((chunk, depth), lambda i, _: (i, 0))
    line_block = pl.BlockSpec((chunk * lines, LANES), lambda i, _: (i, 0))
    out = pl.pallas_call(
        lambda *refs: update_kernel(column_count, *refs),
        out_shape=jax.ShapeDtypeStruct(flat.shape, jnp.float32),
        grid_spec=pltpu.PrefetchScalarGridSpec(
            num_scalar_prefetch=1,
            grid=(rows // chunk,),
            in_specs=[
                line_block, part, part, whole, whole, pl.BlockSpec((chunk, NB), lambda i, _: (i, 0))
            ],
            out_specs=line_block,
        ),
        compiler_params=pltpu.CompilerParams(vmem_limit_bytes=60 * 2**20),
        name="update",
    )(place, flat, row_high, row_low, col_high, col_low, fresh)
    return out.reshape(matrix.shape)


def shards(matrix):
    local_rows = matrix.shape[0]
    local_cols = matrix.shape[3]
    rows = local_rows * NB
    lines = matrix.reshape(rows, local_cols * NB // LANES, LANES)
    mine = lax.optimization_barrier(lines)[:, : NB // LANES].reshape(rows, NB)
    row_count = lax.axis_size("row")
    column_count = lax.axis_size("col")
    group_size = row_count // column_count
    row_place = lax.axis_index("row")
    column_place = lax.axis_index("col")
    tile_rows = jnp.arange(local_rows, dtype=jnp.int32) * row_count + row_place

    corner = mine[:NB]
    at = lambda p, q: (row_place == p) & (column_place == q)
    lead = jnp.stack([jnp.where(at(p, q), corner, 0.0) for p, q in ((0, 0), (1, 0), (1, 1))])
    lead = lax.psum(lead, ("row", "col"))

    swapped = lax.ppermute(mine, "col", [(0, 1), (1, 0)])
    crossed = lax.ppermute(mine, "col", [(0, 2), (1, 3)])
    partner = lax.ppermute(crossed, "col", [(2, 3), (3, 2)])
    near = column_place < 2
    own_half = jnp.where(near, mine, crossed)
    other_half = jnp.where(near, swapped, partner)
    even = column_place % 2 == 0
    raw = jnp.concatenate(
        [jnp.where(even, own_half, other_half), jnp.where(even, other_half, own_half)], axis=1
    )

    pieces = raw.reshape(column_count, rows // column_count, 2 * NB)
    part = row_place % column_count
    piece = lax.dynamic_index_in_dim(pieces, part, 0, keepdims=False)
    for shift in range(1, column_count):
        pairs = [
            (
                (h * column_count + q) * column_count + q,
                (h * column_count + (q + shift) % column_count) * column_count + q,
            )
            for h in range(group_size)
            for q in range(column_count)
        ]
        send = lax.dynamic_index_in_dim(
            pieces, (column_place + shift) % column_count, 0, keepdims=False
        )
        got = lax.ppermute(send, ("row", "col"), pairs)
        piece = jnp.where(part == (column_place + shift) % column_count, got, piece)
    gathered = lax.all_gather(piece, "row", axis=0)

    factor_0, inverse_0, below, factor_1, inverse_1 = factor_lead(lead)

    def solve(panel):
        first = dot_nt(panel[:, :NB], inverse_0, HIGHEST)
        rest = panel[:, NB:] - dot_nt(first, below, HIGHEST)
        return first, dot_nt(rest, inverse_1, HIGHEST)

    first, second = (x.reshape(local_rows, NB, NB) for x in solve(raw))
    row_id = tile_rows[:, None, None]
    column_0 = jnp.where(row_id == 0, factor_0, first)
    column_1 = jnp.where(row_id == 0, 0.0, jnp.where(row_id == 1, factor_1, second))
    row_panel = jnp.concatenate([first, second], axis=2).reshape(rows, 2 * NB)
    fresh = jnp.where(column_place == 0, column_0, column_1).reshape(rows, NB)

    ordered = gathered.reshape(group_size, local_rows, NB, 2 * NB).transpose(1, 0, 2, 3)
    column_panel = jnp.concatenate(solve(ordered.reshape(local_cols * NB, 2 * NB)), axis=1)
    place = jnp.stack([row_place, column_place]).astype(jnp.int32)
    return update(place, lines, row_panel, column_panel, fresh, column_count).reshape(matrix.shape)


def solution(mesh):
    in_specs = (P(None, "row", None, None, "col", None),)
    out_specs = P(None, "row", None, None, "col", None)
    return jax.shard_map(shards, mesh=mesh, in_specs=in_specs, out_specs=out_specs, check_vma=False)
```

time: 1580 us -> 867 us (0.55)
  waiting for transfers between devices: 745 us -> 414 us
  local copies, waits for them, and re-layouts: 321 us -> 41.3 us
  other arithmetic: 302 us -> 37.2 us
  Pallas kernels: 0 us -> 237 us
  matrix products: 165 us -> 94.2 us
  starting transfers between devices: 0.21 us -> 21.9 us
    psum x6 -> x1, waiting for transfers between devices: 745 us -> 279 us  [shards(): lead = lax.psum(lead, ('row', 'col'))]
    pallas_call x0 -> x2, Pallas kernels: none -> 237 us  [the longest x1 140 us: factor_lead(): pl.pallas_call(factor_kernel, out_shape=[tile] * 5, in_specs=[pl.BlockSpe...]
    another operation x34 -> x2, other arithmetic: 240 us -> 3.81 us  [the longest x1 3.26 us: shards(): jnp.stack([jnp.where(at(p, q), corner, 0.0) for p, q in ((0, 0), (1, 0),...]
    reshape x4 -> x0, local copies, waits for them, and re-layouts: 167 us -> none  [the longest x1 78.7 us: shards(): blocks = matrix.reshape(local_rows, NB, local_cols, NB)]
    ppermute x0 -> x6, waiting for transfers between devices: none -> 135 us  [the longest x1 86.2 us: shards(): crossed = lax.ppermute(mine, 'col', [(0, 2), (1, 3)])]
    unnamed x13 -> x31, local copies, waits for them, and re-layouts: 80.5 us -> 6.8 us
    another operation x26 -> x0, matrix products: 39.5 us -> none  [the longest x14 35.7 us: shards(): jax.scipy.linalg.solve_triangular(factor_diag_block, source.reshape(local...]
    dot_general x2 -> x6, matrix products: 126 us -> 94.2 us  [dot_nt(): lax.dot_general(a, b, (((1,), (1,)), ((), ())), precision=precision, pref...]
  transfers between devices with their start and end apart: 6 -> 8, of which waited for: 5 -> 5; matrix products, arithmetic and copies ran while one was open for 8% -> 7% of each run, Pallas kernels for 0% -> 16%
where the time goes in v1:
time: 867 us; the launch traced here: 861 us
  waiting for transfers between devices  414 us (48%)
  Pallas kernels  237 us (27%)
  matrix products  94.2 us (11%)
  local copies, waits for them, and re-layouts  41.3 us (5%)
  other arithmetic  37.2 us (4%)
  starting transfers between devices  21.9 us (3%)
  between operations  15.5 us (2%)
    psum x1, waiting for transfers between devices, shards(): lead = lax.psum(lead, ('row', 'col'))  279 us
    pallas_call x1, Pallas kernels, factor_lead(): pl.pallas_call(factor_kernel, out_shape=[tile] * 5, in_specs=[pl.BlockSpe...  140 us
    pallas_call x1, Pallas kernels, update(): pl.pallas_call(lambda *refs: update_kernel(column_count, *refs), out_shap...  97.4 us
    dot_general x6, matrix products, dot_nt(): lax.dot_general(a, b, (((1,), (1,)), ((), ())), precision=precision, pref...  94.2 us
    ppermute x1, waiting for transfers between devices, shards(): crossed = lax.ppermute(mine, 'col', [(0, 2), (1, 3)])  86.2 us
    ppermute x3, waiting for transfers between devices, shards(): got = lax.ppermute(send, ('row', 'col'), pairs)  48.8 us
  transfers between devices with their start and end apart: 8, of which 5 were waited for; matrix products, arithmetic and copies ran while one was open for 7% of the time, Pallas kernels for 16%

profile of v1, /device:TPU:0, one launch (start us, length us, event | category | flops | bytes accessed | tf_op | source)
XLA Modules:
  0.0 861.2 jit_solution(11737959378310926387)
XLA Ops:
  7.4 3.8 slice.18
  11.1 0.0 copy-start.3
  11.2 2.7 copy.34
  13.9 0.6 copy-done.3
  14.5 6.9 collective-permute-start
  21.4 1.9 collective-permute-start.1
  23.3 86.2 %collective-permute-done = f32[2048,512]{1,0:T(8,128)} collective-permute-done((f32[2048,512]{1,0:T(8,128)}, f32[2048,512]{1,0:T(8,128)}, u32[]{:S(2)}, u32[]{:S(2)}) %collective-permute-start) | collective-permute-done | bytes 4194336 | tf_op jit(solution)/shard_map/ppermute | solution.py:159
  109.5 2.6 collective-permute-start.2
  112.1 0.0 collective-permute-done.1
  112.1 0.0 collective-permute-done.2
  112.1 7.5 broadcast_select_fusion.3
  119.6 8.4 pad_maximum_fusion.2
  128.0 5.8 dynamic-slice_bitcast_fusion
  133.8 4.7 collective-permute-start.5
  138.6 2.6 collective-permute-start.4
  141.2 2.7 collective-permute-start.3
  143.8 2.0 slice_select_fusion.2
  145.9 1.4 select_n.165
  147.3 1.4 select_n.168
  148.7 0.4 select_n.171
  149.1 3.3 pad_maximum_fusion.3
  152.4 0.0 all-reduce.2.cloned.1.call-update
  152.4 0.5 all-gather.3.cloned.1.call-start
  153.0 8.1 collective-permute-done.5
  161.1 2.6 collective-permute-done.4
  163.7 38.1 %collective-permute-done.3 = f32[512,1024]{1,0:T(8,128)} collective-permute-done((f32[512,1024]{1,0:T(8,128)}, f32[512,1024]{1,0:T(8,128)}, u32[]{:S(2)}, u32[]{:S(2)}) %collective-permute-start.3) | collective-permute-done | bytes 2097184 | tf_op jit(solution)/shard_map/ppermute | solution.py:184
  201.8 4.1 fusion.10
  205.9 0.0 all-gather.3.cloned.1.call-update
  205.9 0.1 broadcast_bitcast_fusion
  206.0 0.1 broadcast_bitcast_fusion.1
  206.1 0.6 pad_add_fusion.refs_0_
  206.7 278.7 %all-reduce.2.cloned.1.call-done.lead = f32[3,512,512]{2,1,0:T(8,128)} async-done(((f32[3,512,512]{2,1,0:T(8,128)}), f32[3,512,512]{2,1,0:T(8,128)}) %all-reduce.2.cloned.1.call-update) | async-done | bytes 3145744 | tf_op jit(solution)/shard_map/psum | solution.py:156
  485.4 140.0 %factor_lead.1 = (f32[512,512]{1,0:T(8,128)}, f32[512,512]{1,0:T(8,128)}, f32[512,512]{1,0:T(8,128)}, f32[512,512]{1,0:T(8,128)}, f32[512,512]{1,0:T(8,128)}) custom-call(f32[3,512,512]{2,1,0:T(8,128)} %all-reduce.2.cloned.1.call-done.lead), custom_call_target="tpu_custom_call" | custom-call | flops 99999997952 | bytes 10000000 | tf_op jit(solution)/shard_map/factor_lead/pallas_call | solution.py:71
  625.4 10.4 %fusion.13 = f32[2048,512]{0,1:T(8,128)} fusion(f32[2048,512]{1,0:T(8,128)} %copy-done.2, f32[512,512]{1,0:T(8,128)} %get-tuple-element.10), kind=kOutput, calls=%fused_computation.40 | convolution fusion | flops 6442450944 | bytes 9437184 | tf_op jit(solution)/shard_map/dot_general | solution.py:15
  635.7 5.5 copy.16
  641.3 15.1 %fusion.14 = f32[2048,512]{1,0:T(8,128)S(1)} fusion(f32[2048,512]{0,1:T(8,128)} %fusion.13, f32[512,512]{1,0:T(8,128)S(1)} %copy-done.9), kind=kOutput, calls=%fused_computation.41 | convolution fusion | flops 6442450944 | bytes 9437184 | tf_op jit(solution)/shard_map/dot_general | solution.py:15
  656.5 9.2 %fusion.6 = (f32[2048,512]{1,0:T(8,128)}, f32[2048,512]{1,0:T(8,128)S(1)}) fusion(f32[2048,512]{1,0:T(8,128)S(1)} %copy-done.5, f32[512,512]{1,0:T(8,128)S(1)} %copy-done.12, f32[512,512]{1,0:T(8,128)S(1)} %copy-done.11, pred[2048]{0:T(1024)(128)(4,1)S(1)} %bitcast.65, pred[2048]{0:T(1024)(128)(4,1)S(1)} %bitcast.66, pred[]{:T(512)S(6)} %eq.55, ...), kind=kOutput, calls=%fused_computation.16 | convolution fusion | flops 6447693824 | bytes 24121344 | tf_op jit(solution)/shard_map/dot_general | solution.py:15
  665.7 4.2 fusion.1
  669.8 7.0 copy.18
  676.9 0.0 copy-start.1
  676.9 13.4 %fusion.3 = f32[4096,512]{0,1:T(8,128)S(1)} fusion(f32[512,512]{1,0:T(8,128)S(1)} %copy-done.10, f32[4096,1024]{1,0:T(8,128)S(1)} %bitcast.55), kind=kOutput, calls=%fused_computation.9 | convolution fusion | flops 12884901888 | bytes 17825792 | tf_op jit(solution)/shard_map/dot_general | solution.py:15
  690.4 0.0 copy-done.1
  690.4 3.3 copy-done
  693.7 28.7 %fusion.15 = f32[4096,512]{1,0:T(8,128)} fusion(f32[4096,512]{0,1:T(8,128)S(1)} %fusion.3, f32[512,512]{1,0:T(8,128)S(1)} %copy-done.9), kind=kOutput, calls=%fused_computation.42 | convolution fusion | flops 12884901888 | bytes 17825792 | tf_op jit(solution)/shard_map/dot_general | solution.py:15
  722.4 9.1 %copy.19 = f32[4096,512]{1,0:T(8,128)} copy(f32[4096,512]{0,1:T(8,128)} %copy-done) | data formatting | bytes 16777216 | tf_op jit(solution)/shard_map/dot_general | solution.py:15
  731.4 17.4 %fusion.2 = f32[4096,512]{1,0:T(8,128)S(1)} fusion(f32[512,512]{1,0:T(8,128)S(1)} %copy-done.7, f32[4096,512]{1,0:T(8,128)} %fusion.15, f32[4096,1024]{1,0:T(8,128)} %bitcast.56), kind=kOutput, calls=%fused_computation.8 | convolution fusion | flops 12886999040 | bytes 26214400 | tf_op jit(solution)/shard_map/dot_general | solution.py:15
  748.9 7.1 fusion
  756.0 97.4 %update.1 = f32[65536,128]{1,0:T(8,128)} custom-call(s32[2]{0:T(128)} %pad_add_fusion.refs_0_, f32[65536,128]{1,0:T(8,128)} %bitcast.59, bf16[2048,1024]{1,0:T(8,128)(2,1)} %get-tuple-element.26.refs_2_, bf16[2048,1024]{1,0:T(8,128)(2,1)} %get-tuple-element.25.refs_3_, bf16[4096,1024]{1,0:T(8,128)(2,1)} %get-tuple-element.19.refs_4_, ...), custom_call_target="tpu_custom_call" | custom-call | tf_op jit(solution)/shard_map/update/pallas_call | solution.py:123
  (26 shorter events, 0.1 us)
Async XLA Ops:
  7.4 478.0 %all-reduce.2.cloned.1.call-start = ((), (), s32[]{:S(2)}) async-start(), calls=%async_computation | async-start | bytes 6291456 | tf_op jit(solution)/shard_map/psum | solution.py:156
  11.1 3.3 copy-start.3
  14.5 95.0 %collective-permute-start = (f32[2048,512]{1,0:T(8,128)}, f32[2048,512]{1,0:T(8,128)}, u32[]{:S(2)}, u32[]{:S(2)}) collective-permute-start(f32[2048,512]{1,0:T(8,128)} %bitcast.54), channel_id=1, source_target_pairs={{0,2},{1,3},{4,6},{5,7},{8,10},{9,11},{12,14},{13,15},{16,18},{17,... | collective-permute-start | bytes 12582920 | tf_op jit(solution)/shard_map/ppermute | solution.py:159
  21.4 90.7 %collective-permute-start.1 = (f32[2048,512]{1,0:T(8,128)}, f32[2048,512]{1,0:T(8,128)}, u32[]{:S(2)}, u32[]{:S(2)}) collective-permute-start(f32[2048,512]{1,0:T(8,128)} %bitcast.54), channel_id=1, source_target_pairs={{0,1},{1,0},{4,5},{5,4},{8,9},{9,8},{12,13},{13,12},{16,17},{17,16... | collective-permute-start | bytes 12582920 | tf_op jit(solution)/shard_map/ppermute | solution.py:158
  109.5 2.6 collective-permute-start.2
  119.6 8.4 copy-start.2
  133.8 27.3 %collective-permute-start.5 = (f32[512,1024]{1,0:T(8,128)}, f32[512,1024]{1,0:T(8,128)}, u32[]{:S(2)}, u32[]{:S(2)}) collective-permute-start(f32[512,1024]{1,0:T(8,128)} %get-tuple-element.22), channel_id=1, source_target_pairs={{0,4},{5,9},{10,14},{15,3},{16,20},{21,25},{26,30},{31,19}} | collective-permute-start | bytes 6291464 | tf_op jit(solution)/shard_map/ppermute | solution.py:184
  138.6 25.1 %collective-permute-start.4 = (f32[512,1024]{1,0:T(8,128)}, f32[512,1024]{1,0:T(8,128)}, u32[]{:S(2)}, u32[]{:S(2)}) collective-permute-start(f32[512,1024]{1,0:T(8,128)} %get-tuple-element.23), channel_id=1, source_target_pairs={{0,8},{5,13},{10,2},{15,7},{16,24},{21,29},{26,18},{31,23}} | collective-permute-start | bytes 6291464 | tf_op jit(solution)/shard_map/ppermute | solution.py:184
  141.2 60.6 %collective-permute-start.3 = (f32[512,1024]{1,0:T(8,128)}, f32[512,1024]{1,0:T(8,128)}, u32[]{:S(2)}, u32[]{:S(2)}) collective-permute-start(f32[512,1024]{1,0:T(8,128)} %get-tuple-element.24), channel_id=1, source_target_pairs={{0,12},{5,1},{10,6},{15,11},{16,28},{21,17},{26,22},{31,27}} | collective-permute-start | bytes 6291464 | tf_op jit(solution)/shard_map/ppermute | solution.py:184
  147.3 1.9 copy-start.8
  152.4 517.4 %all-gather.3.cloned.1.call-start = ((), (), s32[]{:S(2)}) async-start(), calls=%async_computation.1 | async-start | bytes 18874368 | tf_op jit(solution)/shard_map/all_gather | solution.py:186
  635.7 5.5 copy-start.9
  641.3 15.2 %copy-start.4 = (f32[2048,512]{1,0:T(8,128)S(1)}, f32[2048,512]{1,0:T(8,128)}, u32[]{:S(2)}) copy-start(f32[2048,512]{1,0:T(8,128)} %get-tuple-element.21) | copy-start | bytes 12582916
  641.3 15.2 %copy-start.5 = (f32[2048,512]{1,0:T(8,128)S(1)}, f32[2048,512]{1,0:T(8,128)}, u32[]{:S(2)}) copy-start(f32[2048,512]{1,0:T(8,128)} %copy.16) | copy-start | bytes 12582916
  641.3 15.2 %copy-start.7 = (f32[512,512]{1,0:T(8,128)S(1)}, f32[512,512]{1,0:T(8,128)}, u32[]{:S(2)}) copy-start(f32[512,512]{1,0:T(8,128)} %get-tuple-element.12) | copy-start | bytes 3145732
  641.3 15.2 %copy-start.11 = (f32[512,512]{1,0:T(8,128)S(1)}, f32[512,512]{1,0:T(8,128)}, u32[]{:S(2)}) copy-start(f32[512,512]{1,0:T(8,128)} %get-tuple-element.13) | copy-start | bytes 3145732
  641.3 15.2 %copy-start.12 = (f32[512,512]{1,0:T(8,128)S(1)}, f32[512,512]{1,0:T(8,128)}, u32[]{:S(2)}) copy-start(f32[512,512]{1,0:T(8,128)} %get-tuple-element.14) | copy-start | bytes 3145732
  669.8 7.1 copy-start.10
  676.9 13.5 %copy-start.1 = (f32[4,2,512,1024]{3,2,1,0:T(8,128)}, f32[4,2,512,1024]{3,2,1,0:T(8,128)S(1)}, u32[]{:S(2)}) copy-start(f32[4,2,512,1024]{3,2,1,0:T(8,128)S(1)} %copy.18) | copy-start | bytes 50331652
  690.4 3.3 copy-start
  731.4 17.4 %copy-start.6 = (f32[4096,512]{1,0:T(8,128)S(1)}, f32[4096,512]{1,0:T(8,128)}, u32[]{:S(2)}) copy-start(f32[4096,512]{1,0:T(8,128)} %copy.19) | copy-start | bytes 25165828
Sparse Core Ops, SparseCore 0:
  152.5 332.7 all-reduce.1
Sparse Core Ops, SparseCore 1:
  206.0 243.1 all-gather.2
